TPU v7x, 32 devices: a whole 2x2x4 slice. The times are simulated.
32 devices in a mesh: seq: 16 (over z, y, x), tp: 2 (over core).
Axes of the slice: x: 2, y: 2, z: 4, core: 2. Of those that a mesh axis runs over, the one named last changes fastest.
Arguments:
- img: bfloat16 [4, 512, 3072], P(None, 'seq', 'tp'), may hold values from -6 to 6
- txt: bfloat16 [4, 64, 3072], P(None, 'seq', 'tp'), may hold values from -6 to 6
- prev_mod: bfloat16 [4, 512, 3072], P(None, 'seq', 'tp'), may hold values from -47 to 47
- cache: float32 [4, 512, 3072], P(None, 'seq', 'tp'), may hold values from -6 to 6
- modulation: bfloat16 [3, 4, 3072], P(None, None, 'tp'), may hold values from -4 to 4
- w_qkv: bfloat16 [3072, 3, 2048], P('seq', None, 'tp'), may hold values from -1 to 1, as said below
- qk_gain: float32 [2, 2048], P(None, 'tp'), may hold values from 0.5 to 6, as said below
- output_weight: bfloat16 [2048, 3072], P('tp'), may hold values from -0.1875 to 0.1875
- text_len: int32 [4], replicated, may hold values from 1 to 64
- refresh: int32 [4], replicated, may hold values from 0 to 1, as said below
Outputs:
- out_img: float32 [4, 512, 3072], P(None, 'seq', 'tp')
- new_cache: float32 [4, 512, 3072], P(None, 'seq', 'tp')
- rel_l1: float32 [4], replicated
Inputs may be any that keep to these rules, and one draw needn't show every extreme that they name: `refresh`: at least one sequence has flag 1 and at least one has flag 0. `w_qkv`: entries of spread about one over the square root of 3072. `qk_gain`: positive.
All inputs are finite; a program needn't handle non-finite values.
Results may differ from a plain program's by a relative error of at most 0.013.
The roundings to bfloat16 on the way count: a program that leaves them out, or rounds other values in their place, can miss the bound.
Values may be sent and summed in bfloat16 or wider, within the bound.
A program may use at most 128 MiB of HBM per device.

v0:
```python
import jax
import jax.numpy as jnp
from jax import lax
from jax.sharding import PartitionSpec as P

HD = 128
EPS = 0.1
NEG = -1e30


def unit_heads(block, gain):
    shaped = block.reshape(block.shape[:-1] + (block.shape[-1] // HD, HD))
    scaled = shaped * lax.rsqrt(jnp.mean(jnp.square(shaped), axis=-1, keepdims=True) + EPS)
    return scaled.reshape(block.shape) * gain


def local(img, txt, prev_mod, cache, modulation, w_qkv, qk_gain, output_weight, text_len, refresh):
    batch, img_rows, width_loc = img.shape
    txt_rows = txt.shape[1]
    rows = txt_rows + img_rows
    joined = jnp.concatenate([txt, img], axis=1)
    local_mods = modulation.astype(jnp.float32)
    wide, wide_mod = (
        lax.all_gather(joined, "tp", axis=2, tiled=True),
        lax.all_gather(modulation, "tp", axis=2, tiled=True),
    )
    wide_mods = wide_mod.astype(jnp.float32)
    values = wide.astype(jnp.float32)
    center = jnp.mean(values, axis=2, keepdims=True)
    spread = jnp.mean(jnp.square(values - center), axis=2, keepdims=True)
    normed = (values - center) * lax.rsqrt(spread + EPS)
    modded = (normed * (1.0 + wide_mods[1][:, None, :]) + wide_mods[0][:, None, :]).astype(
        jnp.bfloat16
    )
    offset = lax.axis_index("tp") * width_loc
    own_image = lax.dynamic_slice_in_dim(modded[:, txt_rows:, :], offset, width_loc, 2)
    previous = prev_mod.astype(jnp.float32)
    gap = jnp.sum(jnp.abs(own_image.astype(jnp.float32) - previous), axis=(1, 2))
    base_sum = jnp.sum(jnp.abs(previous), axis=(1, 2))
    numer, denom = lax.psum((gap, base_sum), ("seq", "tp"))
    rel_l1 = numer / jnp.maximum(denom, 1.0)
    columns = w_qkv.shape[2]
    projected = jnp.einsum(
        "btd,dkc->btkc",
        modded,
        lax.all_gather(w_qkv, "seq", axis=0, tiled=True),
        preferred_element_type=jnp.float32,
    )
    heads = columns // HD
    query = unit_heads(projected[:, txt_rows:, 0, :], qk_gain[0]).astype(jnp.bfloat16)
    query_heads = query.reshape(batch, img_rows, heads, HD)
    keyed = unit_heads(projected[:, :, 1, :], qk_gain[1]).astype(jnp.bfloat16)
    valued = projected[:, :, 2, :].astype(jnp.bfloat16)
    paired = jnp.stack([keyed, valued], axis=2)
    score_scale = 1.0 / HD**0.5
    start_top = jnp.full((batch, heads, img_rows), NEG, jnp.float32)
    piece = lax.all_gather(paired, "seq", axis=1, tiled=True)
    top = start_top
    count = piece.shape[1]
    index = jnp.arange(count, dtype=jnp.int32)
    slot = index % rows
    text_pos = index // rows * txt_rows + slot
    valid = (slot >= txt_rows)[None, :] | (text_pos[None, :] < text_len[:, None])
    keys = piece[:, :, 0, :].reshape(batch, count, heads, HD)
    vals = piece[:, :, 1, :].reshape(batch, count, heads, HD)
    logit_scores = (
        jnp.einsum("bqhc,bkhc->bhqk", query_heads, keys, preferred_element_type=jnp.float32)
        * score_scale
    )
    logit_scores = jnp.where(valid[:, None, None, :], logit_scores, NEG)
    new_top = jnp.maximum(top, jnp.max(logit_scores, axis=3))
    attention_weights = jnp.where(
        valid[:, None, None, :], jnp.exp(logit_scores - new_top[..., None]), 0.0
    )
    total = jnp.sum(attention_weights, axis=3)
    summed_output = jnp.einsum(
        "bhqk,bkhc->bhqc",
        attention_weights.astype(jnp.bfloat16),
        vals,
        preferred_element_type=jnp.float32,
    )
    top, total, summed_output = (new_top, total, summed_output)
    attended_values = (summed_output / total[..., None]).astype(jnp.bfloat16)
    attended_values = attended_values.transpose(0, 2, 1, 3).reshape(batch, img_rows, columns)
    partial_output = jnp.einsum(
        "pxr,ro->pxo", attended_values, output_weight, preferred_element_type=jnp.float32
    )
    whole = lax.psum(partial_output.astype(jnp.bfloat16), "tp").astype(jnp.float32)
    mixed_heads = lax.dynamic_slice_in_dim(whole, lax.axis_index("tp") * width_loc, width_loc, 2)
    resid = local_mods[2][:, None, :] * mixed_heads
    flag = (refresh == 1)[:, None, None]
    new_cache = jnp.where(flag, resid, cache)
    out_img = img.astype(jnp.float32) + new_cache
    return (out_img, new_cache, rel_l1)


def solution(mesh):
    return jax.shard_map(
        local,
        mesh=mesh,
        in_specs=(
            P(None, "seq", "tp"),
            P(None, "seq", "tp"),
            P(None, "seq", "tp"),
            P(None, "seq", "tp"),
            P(None, None, "tp"),
            P("seq", None, "tp"),
            P(None, "tp"),
            P("tp", None),
            P(),
            P(),
        ),
        out_specs=(P(None, "seq", "tp"), P(None, "seq", "tp"), P()),
        check_vma=False,
    )
```

profile of v0, /device:TPU:0, one launch (start us, length us, event | category | flops | bytes accessed | tf_op | source)
XLA Modules:
  0.0 434.7 jit_solution(10169232465015273428)
XLA Ops:
  7.2 0.0 all-gather.3.cloned.1.call-start
  7.2 0.7 all-gather.3.cloned.1.call-update
  7.9 0.0 all-gather.5.cloned.1.call-start
  8.0 2.2 all_gather.13
  10.2 1.1 pad_maximum_fusion.1
  11.3 2.5 all_gather.12
  13.8 0.2 convert_reduce_fusion
  14.1 0.4 fusion.14
  14.5 0.5 fusion.17
  15.0 209.3 %all-gather.3.cloned.1.call-done = bf16[3072,3,1024]{2,0,1:T(8,128)(2,1)} async-done(((bf16[192,3,1024]{2,0,1:T(8,128)(2,1)}), bf16[3072,3,1024]{2,0,1:T(8,128)(2,1)}) %all-gather.3.cloned.1.call-update) | async-done | bytes 18874384 | tf_op jit(solution)/shard_map/all_gather | solution.py:46
  224.3 8.1 %fusion = f32[4,36,3,1024]{3,1,2,0:T(8,128)S(1)} fusion(bf16[3072,3,1024]{2,0,1:T(8,128)(2,1)} %all-gather.3.cloned.1.call-done, bf16[4,36,3072]{2,1,0:T(8,128)(2,1)S(1)} %fusion.17), kind=kOutput, calls=%fused_computation | convolution fusion | flops 2717908992 | bytes 21528576 | tf_op jit(solution)/shard_map/btd,dkc->btkc/dot_general | solution.py:43
  232.4 0.9 slice_multiply_fusion
  233.3 0.8 slice.62
  234.1 1.2 reshape.130
  235.3 0.9 reduce_sum.66
  236.1 1.0 copy.47
  237.1 0.1 copy.48
  237.2 1.0 mul.103
  238.3 1.3 mul.104
  239.5 0.4 fusion.51
  239.9 0.0 copy-start.2
  239.9 1.1 pad_maximum_fusion
  241.0 1.3 copy.50
  242.3 0.0 all-gather.5.cloned.1.call-update
  242.3 0.0 all-reduce.3.cloned.1.call-start
  242.4 1.1 slice.53
  243.5 1.3 fusion.49
  244.8 40.5 %all-reduce = (f32[4]{0:T(128)S(1)}, f32[4]{0:T(128)S(1)}) all-reduce(f32[4]{0:T(128)S(1)} %get-tuple-element.4, f32[4]{0:T(128)S(1)} %get-tuple-element.3), channel_id=1, replica_groups=mesh['seq'=16,'tp'=2] {'seq','tp'}, use_global_device_ids=true, to_apply=%region_8.9 | all-reduce | flops 8 | bytes 64 | tf_op jit(solution)/shard_map/psum | solution.py:40
  285.3 0.1 compare_or_fusion
  285.4 0.1 slice.48
  285.5 0.1 copy.66
  285.6 0.2 fusion.52
  285.8 0.2 fusion.54
  286.0 77.3 %all-gather.5.cloned.1.call-done = bf16[4,576,2,1024]{3,0,2,1:T(4,128)(2,1)} async-done(((bf16[4,36,2,1024]{3,0,2,1:T(4,128)(2,1)}), bf16[4,576,2,1024]{3,0,2,1:T(4,128)(2,1)}) %all-gather.5.cloned.1.call-update) | async-done | bytes 9437200 | tf_op jit(solution)/shard_map/all_gather | solution.py:57
  363.3 10.7 %fusion.70 = (bf16[4,576,1,1024]{3,0,2,1:T(4,128)(2,1)}, bf16[4,576,1,1024]{3,0,2,1:T(4,128)(2,1)}) fusion(bf16[4,576,2,1024]{3,0,2,1:T(4,128)(2,1)} %all-gather.5.cloned.1.call-done), kind=kLoop, calls=%fused_computation.82 | loop fusion | bytes 18874368 | tf_op jit(solution)/shard_map/slice | solution.py:64
  374.0 8.0 %reshape.131 = bf16[4,576,8,128]{3,2,0,1:T(8,128)(2,1)} reshape(bf16[4,576,1,1024]{3,0,2,1:T(4,128)(2,1)} %get-tuple-element.9) | data formatting | bytes 9437184 | tf_op jit(solution)/shard_map/reshape;squeeze | solution.py:64
  382.0 7.5 %fusion.13 = (f32[4,8,32]{2,1,0:T(8,128)S(1)}, f32[4,8,32,576]{3,2,1,0:T(8,128)S(1)}) fusion(pred[4,576]{1,0:T(4,128)(4,1)S(1)} %compare_or_fusion, bf16[4,576,8,128]{3,2,0,1:T(8,128)(2,1)} %reshape.131, bf16[4,32,8,128]{3,2,1,0:T(8,128)(2,1)S(1)} %fusion.54), kind=kOutput, calls=%fused_computation.15 | convolution fusion | flops 152763392 | bytes 7346432 | tf_op jit(solution)/shard_map/bqhc,bkhc->bhqk/dot_general | solution.py:67
  389.5 8.0 %reshape.132 = bf16[4,576,8,128]{3,2,0,1:T(8,128)(2,1)} reshape(bf16[4,576,1,1024]{3,0,2,1:T(4,128)(2,1)} %get-tuple-element.10) | data formatting | bytes 9437184 | tf_op jit(solution)/shard_map/reshape;squeeze | solution.py:65
  397.6 0.8 fusion.18
  398.4 0.0 slice-start.1
  398.4 8.1 %fusion.41 = bf16[4,8,4,8,128]{4,3,2,1,0:T(8,128)(2,1)S(1)} fusion(bf16[4,576,8,128]{3,2,0,1:T(8,128)(2,1)} %reshape.132, f32[4,8,32,576]{3,2,1,0:T(8,128)S(1)} %get-tuple-element.16, f32[4,8,32]{2,1,0:T(8,128)S(1)} %broadcast_maximum_fusion, pred[4,576]{1,0:T(4,128)(4,1)S(1)} %compare_or_fusion, f32[4,32,8]{1,2,0:T(8,128)S(1)} %bitcast.67), kind=kOutput, calls=%fused_computation.30 | convolution fusion | flops 154206208 | bytes 7350528 | tf_op jit(solution)/shard_map/bhqk,bkhc->bhqc/dot_general | solution.py:76
  406.6 0.0 copy-start.1
  406.6 1.9 fusion.8
  408.4 0.0 all-reduce.3.cloned.1.call-update
  408.5 0.5 maximum_divide_fusion
  409.0 0.7 bitcast_convert_fusion
  409.7 16.1 %all-reduce.3.cloned.1.call-done = bf16[4,32,3072]{2,1,0:T(8,128)(2,1)} async-done(((bf16[4,32,3072]{2,1,0:T(8,128)(2,1)}), bf16[4,32,3072]{2,1,0:T(8,128)(2,1)}) %all-reduce.3.cloned.1.call-update) | async-done | bytes 786448 | tf_op jit(solution)/shard_map/psum | solution.py:88
  425.8 2.4 convert_add_fusion
  (25 shorter events, 0.1 us)
Async XLA Ops:
  7.2 217.1 %all-gather.3.cloned.1.call-start = ((), (), s32[]{:S(2)}) async-start(), calls=%async_computation | async-start | bytes 20054016 | tf_op jit(solution)/shard_map/all_gather | solution.py:46
  7.9 6.6 %copy-start.3 = (f32[2,1024]{1,0:T(2,128)S(1)}, f32[2,1024]{1,0:T(2,128)}, u32[]{:S(2)}) copy-start(f32[2,1024]{1,0:T(2,128)} %param.16) | copy-start | bytes 24580
  7.9 355.4 %all-gather.5.cloned.1.call-start = ((), (), s32[]{:S(2)}) async-start(), calls=%async_computation.1 | async-start | bytes 10027008 | tf_op jit(solution)/shard_map/all_gather | solution.py:57
  239.9 3.6 copy-start.2
  239.9 45.4 %copy-start.4 = (s32[4]{0:T(128)S(1)}, s32[4]{0:T(128)}, u32[]{:S(2)}) copy-start(s32[4]{0:T(128)} %param.18) | copy-start | bytes 52
  242.3 183.5 %all-reduce.3.cloned.1.call-start = ((), (), s32[]{:S(2)}) async-start(), calls=%async_computation.2 | async-start | bytes 1572864 | tf_op jit(solution)/shard_map/psum | solution.py:88
  397.6 8.9 %slice-start = ((s8[6291456]{0:T(1024)(128)(4,1)}), s8[4194304]{0:T(1024)(128)(4,1)S(1)}, s32[]{:S(2)}) async-start(s8[6291456]{0:T(1024)(128)(4,1)} %bitcast.62), calls=%async_computation.3 | async-start | bytes 8388608
  398.4 8.1 %slice-start.1 = ((s8[6291456]{0:T(1024)(128)(4,1)}), s8[2097152]{0:T(1024)(128)(4,1)S(1)}, s32[]{:S(2)}) async-start(s8[6291456]{0:T(1024)(128)(4,1)} %bitcast.62), calls=%async_computation.4 | async-start | bytes 4194304
  406.5 1.9 copy-start.5
  406.5 19.2 %copy-start = (bf16[4,32,1536]{2,1,0:T(8,128)(2,1)S(1)}, bf16[4,32,1536]{2,1,0:T(8,128)(2,1)}, u32[]{:S(2)}) copy-start(bf16[4,32,1536]{2,1,0:T(8,128)(2,1)} %param.10) | copy-start | bytes 1179652
  406.6 19.2 %copy-start.1 = (f32[4,32,1536]{2,1,0:T(8,128)S(1)}, f32[4,32,1536]{2,1,0:T(8,128)}, u32[]{:S(2)}) copy-start(f32[4,32,1536]{2,1,0:T(8,128)} %param.13) | copy-start | bytes 2359300
Sparse Core Ops, SparseCore 0:
  10.6 213.6 all-gather.2
  242.4 120.8 all-gather.4
  408.6 17.1 all-reduce.2
where the time goes:
time: 436 us; the launch traced here: 435 us
  waiting for transfers between devices  303 us (69%)
  blocking collectives  45.3 us (10%)
  local copies, waits for them, and re-layouts  34.7 us (8%)
  matrix products  25.6 us (6%)
  between operations  14 us (3%)
  other arithmetic  11.8 us (3%)
    all_gather x1, waiting for transfers between devices, local(): lax.all_gather(w_qkv, 'seq', axis=0, tiled=True)  209 us
    all_gather x1, waiting for transfers between devices, local(): piece = lax.all_gather(paired, 'seq', axis=1, tiled=True)  77.3 us
    psum x1, blocking collectives, local(): numer, denom = lax.psum((gap, base_sum), ('seq', 'tp'))  40.5 us
    psum x1, waiting for transfers between devices, local(): lax.psum(partial_output.astype(jnp.bfloat16), 'tp').astype(jnp.float32)  16.1 us
    slice x1, local copies, waits for them, and re-layouts, local(): keys = piece[:, :, 0, :].reshape(batch, count, heads, HD)  10.7 us
  transfers between devices with their start and end apart: 3, of which 3 were waited for; matrix products, arithmetic and copies ran while one was open for 2% of the time, Pallas kernels for 0%

commit v1 on v0

--- a/solution.py
+++ b/solution.py
@@ -2,6 +2,7 @@
 import jax.numpy as jnp
 from jax import lax
 from jax.sharding import PartitionSpec as P
+from jax.lax import axis_index, axis_size, ppermute
 
 HD = 128
 EPS = 0.1
@@ -40,12 +41,41 @@
     numer, denom = lax.psum((gap, base_sum), ("seq", "tp"))
     rel_l1 = numer / jnp.maximum(denom, 1.0)
     columns = w_qkv.shape[2]
+    local_now, u_next, work_now = (axis_size("seq"), axis_index("seq"), w_qkv.shape[0])
+    entries = tuple(((at, (at + 1) % local_now) for at in range(local_now)))
+    all_rows = tuple(((at, (at - 1) % local_now) for at in range(local_now)))
+    current_block = local_now // 2
+    s_next = t_next = w_qkv
     projected = jnp.einsum(
         "btd,dkc->btkc",
-        modded,
-        lax.all_gather(w_qkv, "seq", axis=0, tiled=True),
+        lax.dynamic_slice_in_dim(modded, u_next * work_now, w_qkv.shape[0], axis=2),
+        w_qkv,
         preferred_element_type=jnp.float32,
     )
+    t = 1
+    while t < current_block + 1:
+        s_next = ppermute(s_next, axis_name="seq", perm=entries)
+        if t < local_now - current_block:
+            t_next = ppermute(t_next, axis_name="seq", perm=all_rows)
+            response = jnp.einsum(
+                "btd,dkc->btkc",
+                lax.dynamic_slice_in_dim(
+                    modded, (u_next + t) % local_now * work_now, t_next.shape[0], axis=2
+                ),
+                t_next,
+                preferred_element_type=jnp.float32,
+            )
+            projected = projected + response
+        near = jnp.einsum(
+            "btd,dkc->btkc",
+            lax.dynamic_slice_in_dim(
+                modded, (u_next - t) % local_now * work_now, s_next.shape[0], axis=2
+            ),
+            s_next,
+            preferred_element_type=jnp.float32,
+        )
+        projected = projected + near
+        t = t + 1
     heads = columns // HD
     query = unit_heads(projected[:, txt_rows:, 0, :], qk_gain[0]).astype(jnp.bfloat16)
     query_heads = query.reshape(batch, img_rows, heads, HD)

time: 436 us -> 607 us (1.39)
  starting transfers between devices: 0.12 us -> 107 us
  waiting for transfers between devices: 303 us -> 349 us
  matrix products: 25.6 us -> 42.6 us
    ppermute x0 -> x15, waiting for transfers between devices: none -> 253 us  [the longest x8 253 us: local(): s_next = ppermute(s_next, axis_name='seq', perm=entries)]
    all_gather x1 -> x0, waiting for transfers between devices: 209 us -> none  [local(): lax.all_gather(w_qkv, 'seq', axis=0, tiled=True)]
    ppermute x0 -> x15, starting transfers between devices: none -> 107 us  [the longest x7 86.2 us: local(): t_next = ppermute(t_next, axis_name='seq', perm=all_rows)]
    dot_general x1 -> x16, matrix products: 8.14 us -> 25.2 us  [the longest x8 16.1 us: local(): jnp.einsum('btd,dkc->btkc', lax.dynamic_slice_in_dim(modded, (u_next - t)...]
  transfers between devices with their start and end apart: 3 -> 17, of which waited for: 3 -> 10; matrix products, arithmetic and copies ran while one was open for 2% -> 4% of each run, Pallas kernels for 0% -> 0%
where the time goes in v1:
time: 607 us; the launch traced here: 606 us
  waiting for transfers between devices  349 us (57%)
  starting transfers between devices  107 us (18%)
  blocking collectives  45.8 us (8%)
  matrix products  42.6 us (7%)
  local copies, waits for them, and re-layouts  35.5 us (6%)
  between operations  14.7 us (2%)
  other arithmetic  11.7 us (2%)
    ppermute x8, waiting for transfers between devices, local(): s_next = ppermute(s_next, axis_name='seq', perm=entries)  253 us
    ppermute x7, starting transfers between devices, local(): t_next = ppermute(t_next, axis_name='seq', perm=all_rows)  86.2 us
    all_gather x1, waiting for transfers between devices, local(): piece = lax.all_gather(paired, 'seq', axis=1, tiled=True)  79.3 us
    psum x1, blocking collectives, local(): numer, denom = lax.psum((gap, base_sum), ('seq', 'tp'))  41.5 us
    ppermute x8, starting transfers between devices, local(): s_next = ppermute(s_next, axis_name='seq', perm=entries)  20.3 us
    dot_general x8, matrix products, local(): jnp.einsum('btd,dkc->btkc', lax.dynamic_slice_in_dim(modded, (u_next - t)...  16.1 us
    psum x1, waiting for transfers between devices, local(): lax.psum(partial_output.astype(jnp.bfloat16), 'tp').astype(jnp.float32)  16.1 us
  transfers between devices with their start and end apart: 17, of which 10 were waited for; matrix products, arithmetic and copies ran while one was open for 4% of the time, Pallas kernels for 0%

profile of v1, /device:TPU:0, one launch (start us, length us, event | category | flops | bytes accessed | tf_op | source)
XLA Modules:
  0.0 605.8 jit_solution(7992602862170081141)
XLA Ops:
  7.2 3.0 collective-permute-start.1
  10.2 4.1 collective-permute-start
  14.3 46.8 %collective-permute-done.1 = bf16[192,3,1024]{2,0,1:T(8,128)(2,1)S(1)} collective-permute-done((bf16[192,3,1024]{2,0,1:T(8,128)(2,1)}, bf16[192,3,1024]{2,0,1:T(8,128)(2,1)S(1)}, u32[]{:S(2)}, u32[]{:S(2)}) %collective-permute-start.1) | collective-permute-done | bytes 1179680 | tf_op jit(solution)/shard_map/ppermute | solution.py:57
  61.1 2.4 collective-permute-start.3
  63.4 3.2 collective-permute-start.2
  66.7 46.4 %collective-permute-done.3 = bf16[192,3,1024]{2,0,1:T(8,128)(2,1)S(1)} collective-permute-done((bf16[192,3,1024]{2,0,1:T(8,128)(2,1)S(1)}, bf16[192,3,1024]{2,0,1:T(8,128)(2,1)S(1)}, u32[]{:S(2)}, u32[]{:S(2)}) %collective-permute-start.3) | collective-permute-done | bytes 1179680 | tf_op jit(solution)/shard_map/ppermute | solution.py:57
  113.1 2.5 collective-permute-start.5
  116.7 2.5 all_gather.9
  119.5 3.2 collective-permute-start.4
  122.6 41.7 %collective-permute-done.5 = bf16[192,3,1024]{2,0,1:T(8,128)(2,1)S(1)} collective-permute-done((bf16[192,3,1024]{2,0,1:T(8,128)(2,1)S(1)}, bf16[192,3,1024]{2,0,1:T(8,128)(2,1)S(1)}, u32[]{:S(2)}, u32[]{:S(2)}) %collective-permute-start.5) | collective-permute-done | bytes 1179680 | tf_op jit(solution)/shard_map/ppermute | solution.py:57
  164.4 2.5 collective-permute-start.7
  166.9 1.8 all_gather.10
  169.2 3.2 collective-permute-start.6
  172.4 43.1 %collective-permute-done.7 = bf16[192,3,1024]{2,0,1:T(8,128)(2,1)} collective-permute-done((bf16[192,3,1024]{2,0,1:T(8,128)(2,1)S(1)}, bf16[192,3,1024]{2,0,1:T(8,128)(2,1)}, u32[]{:S(2)}, u32[]{:S(2)}) %collective-permute-start.7) | collective-permute-done | bytes 1179680 | tf_op jit(solution)/shard_map/ppermute | solution.py:57
  215.5 2.6 collective-permute-start.9
  220.7 24.6 %collective-permute-start.8 = (bf16[192,3,1024]{2,0,1:T(8,128)(2,1)}, bf16[192,3,1024]{2,0,1:T(8,128)(2,1)S(1)}, u32[]{:S(2)}, u32[]{:S(2)}) collective-permute-start(bf16[192,3,1024]{2,0,1:T(8,128)(2,1)} %collective-permute-done.6), channel_id=1, source_target_pairs={{0,30},{2,0},{4,2},{6,4},{8,6},{10,8},{12,10},{14,12},{16,14},{18,... | collective-permute-start | bytes 3538952 | tf_op jit(solution)/shard_map/ppermute | solution.py:59
  245.8 21.0 %collective-permute-done.9 = bf16[192,3,1024]{2,0,1:T(8,128)(2,1)} collective-permute-done((bf16[192,3,1024]{2,0,1:T(8,128)(2,1)}, bf16[192,3,1024]{2,0,1:T(8,128)(2,1)}, u32[]{:S(2)}, u32[]{:S(2)}) %collective-permute-start.9) | collective-permute-done | bytes 1179680 | tf_op jit(solution)/shard_map/ppermute | solution.py:57
  266.7 2.5 collective-permute-start.11
  270.2 1.8 fusion.48
  272.0 24.6 %collective-permute-start.10 = (bf16[192,3,1024]{2,0,1:T(8,128)(2,1)S(1)}, bf16[192,3,1024]{2,0,1:T(8,128)(2,1)S(1)}, u32[]{:S(2)}, u32[]{:S(2)}) collective-permute-start(bf16[192,3,1024]{2,0,1:T(8,128)(2,1)S(1)} %collective-permute-done.8), channel_id=1, source_target_pairs={{0,30},{2,0},{4,2},{6,4},{8,6},{10,8},{12,10},{14,12},{16,14},{18,... | collective-permute-start | bytes 3538952 | tf_op jit(solution)/shard_map/ppermute | solution.py:59
  297.1 20.1 %collective-permute-done.11 = bf16[192,3,1024]{2,0,1:T(8,128)(2,1)S(1)} collective-permute-done((bf16[192,3,1024]{2,0,1:T(8,128)(2,1)}, bf16[192,3,1024]{2,0,1:T(8,128)(2,1)S(1)}, u32[]{:S(2)}, u32[]{:S(2)}) %collective-permute-start.11) | collective-permute-done | bytes 1179680 | tf_op jit(solution)/shard_map/ppermute | solution.py:57
  317.2 2.4 collective-permute-start.13
  319.5 1.7 fusion.44
  321.3 1.7 fusion.42
  323.5 23.4 %collective-permute-start.12 = (bf16[192,3,1024]{2,0,1:T(8,128)(2,1)S(1)}, bf16[192,3,1024]{2,0,1:T(8,128)(2,1)S(1)}, u32[]{:S(2)}, u32[]{:S(2)}) collective-permute-start(bf16[192,3,1024]{2,0,1:T(8,128)(2,1)S(1)} %collective-permute-done.10), channel_id=1, source_target_pairs={{0,30},{2,0},{4,2},{6,4},{8,6},{10,8},{12,10},{14,12},{16,14},{18,... | collective-permute-start | bytes 3538952 | tf_op jit(solution)/shard_map/ppermute | solution.py:59
  347.0 3.0 fusion.38
  350.0 18.5 %collective-permute-done.13 = bf16[192,3,1024]{2,0,1:T(8,128)(2,1)S(1)} collective-permute-done((bf16[192,3,1024]{2,0,1:T(8,128)(2,1)S(1)}, bf16[192,3,1024]{2,0,1:T(8,128)(2,1)S(1)}, u32[]{:S(2)}, u32[]{:S(2)}) %collective-permute-start.13) | collective-permute-done | bytes 1179680 | tf_op jit(solution)/shard_map/ppermute | solution.py:57
  368.5 2.5 collective-permute-start.14
  371.0 1.8 fusion.36
  372.8 1.8 fusion.34
  374.5 1.7 fusion.30
  376.3 1.8 fusion.32
  378.1 15.8 %collective-permute-done.14 = bf16[192,3,1024]{2,0,1:T(8,128)(2,1)} collective-permute-done((bf16[192,3,1024]{2,0,1:T(8,128)(2,1)S(1)}, bf16[192,3,1024]{2,0,1:T(8,128)(2,1)}, u32[]{:S(2)}, u32[]{:S(2)}) %collective-permute-start.14) | collective-permute-done | bytes 1179680 | tf_op jit(solution)/shard_map/ppermute | solution.py:57
  393.8 6.4 %add_add_fusion = f32[4,36,3,1024]{3,1,2,0:T(8,128)S(1)} fusion(f32[4,36,3,1024]{3,1,2,0:T(8,128)} %fusion.30, f32[4,36,3,1024]{3,1,2,0:T(8,128)} %fusion.32, f32[4,36,3,1024]{3,1,2,0:T(8,128)} %fusion.34, f32[4,36,3,1024]{3,1,2,0:T(8,128)} %fusion.36, f32[4,36,3,1024]{3,1,2,0:T(8,128)} %fusion.38, f32[4,36,3,1024]{3,1,2,0:T(8,128)S(1)} %fusion.40, ...), kind=kOutput, calls=%fused_computation.18 | convolution fusion | flops 176504832 | bytes 31539204 | tf_op jit(solution)/shard_map/btd,dkc->btkc/dot_general | solution.py:69
  401.9 1.2 reshape.160
  406.1 1.3 mul.168
  408.8 1.3 copy.50
  411.2 1.3 fusion.77
  412.5 41.5 %all-reduce = (f32[4]{0:T(128)S(1)}, f32[4]{0:T(128)S(1)}) all-reduce(f32[4]{0:T(128)S(1)} %get-tuple-element.4, f32[4]{0:T(128)S(1)} %get-tuple-element.3), channel_id=1, replica_groups=mesh['seq'=16,'tp'=2] {'seq','tp'}, use_global_device_ids=true, to_apply=%region_8.9 | all-reduce | flops 8 | bytes 64 | tf_op jit(solution)/shard_map/psum | solution.py:41
  454.7 79.3 %all-gather.2.cloned.1.call-done = bf16[4,576,2,1024]{3,0,2,1:T(4,128)(2,1)} async-done(((bf16[4,36,2,1024]{3,0,2,1:T(4,128)(2,1)}), bf16[4,576,2,1024]{3,0,2,1:T(4,128)(2,1)}) %all-gather.2.cloned.1.call-update) | async-done | bytes 9437200 | tf_op jit(solution)/shard_map/all_gather | solution.py:87
  534.0 10.7 %fusion.146 = (bf16[4,576,1,1024]{3,0,2,1:T(4,128)(2,1)}, bf16[4,576,1,1024]{3,0,2,1:T(4,128)(2,1)}) fusion(bf16[4,576,2,1024]{3,0,2,1:T(4,128)(2,1)} %all-gather.2.cloned.1.call-done), kind=kLoop, calls=%fused_computation.159 | loop fusion | bytes 18874368 | tf_op jit(solution)/shard_map/slice | solution.py:94
  544.8 8.1 %reshape.161 = bf16[4,576,8,128]{3,2,0,1:T(8,128)(2,1)} reshape(bf16[4,576,1,1024]{3,0,2,1:T(4,128)(2,1)} %get-tuple-element.9) | data formatting | bytes 9437184 | tf_op jit(solution)/shard_map/reshape;squeeze | solution.py:94
  552.8 7.5 %fusion.11 = (f32[4,8,32]{2,1,0:T(8,128)S(1)}, f32[4,8,32,576]{3,2,1,0:T(8,128)S(1)}) fusion(pred[4,576]{1,0:T(4,128)(4,1)S(1)} %compare_or_fusion, bf16[4,576,8,128]{3,2,0,1:T(8,128)(2,1)} %reshape.161, bf16[4,32,8,128]{3,2,1,0:T(8,128)(2,1)S(1)} %fusion.82), kind=kOutput, calls=%fused_computation.13 | convolution fusion | flops 152763392 | bytes 7346432 | tf_op jit(solution)/shard_map/bqhc,bkhc->bhqk/dot_general | solution.py:97
  560.3 8.1 %reshape.162 = bf16[4,576,8,128]{3,2,0,1:T(8,128)(2,1)} reshape(bf16[4,576,1,1024]{3,0,2,1:T(4,128)(2,1)} %get-tuple-element.10) | data formatting | bytes 9437184 | tf_op jit(solution)/shard_map/reshape;squeeze | solution.py:95
  569.2 8.1 %fusion.70 = bf16[4,8,4,8,128]{4,3,2,1,0:T(8,128)(2,1)S(1)} fusion(bf16[4,576,8,128]{3,2,0,1:T(8,128)(2,1)} %reshape.162, f32[4,8,32,576]{3,2,1,0:T(8,128)S(1)} %get-tuple-element.16, f32[4,8,32]{2,1,0:T(8,128)S(1)} %broadcast_maximum_fusion, pred[4,576]{1,0:T(4,128)(4,1)S(1)} %compare_or_fusion, f32[4,32,8]{1,2,0:T(8,128)S(1)} %bitcast.187), kind=kOutput, calls=%fused_computation.60 | convolution fusion | flops 154206208 | bytes 7350528 | tf_op jit(solution)/shard_map/bhqk,bkhc->bhqc/dot_general | solution.py:106
  577.4 1.9 fusion.6
  580.5 16.1 %all-reduce.3.cloned.1.call-done = bf16[4,32,3072]{2,1,0:T(8,128)(2,1)} async-done(((bf16[4,32,3072]{2,1,0:T(8,128)(2,1)}), bf16[4,32,3072]{2,1,0:T(8,128)(2,1)}) %all-reduce.3.cloned.1.call-update) | async-done | bytes 786448 | tf_op jit(solution)/shard_map/psum | solution.py:118
  596.6 2.4 convert_add_fusion
  (87 shorter events, 16.5 us)
Async XLA Ops:
  7.2 159.7 %copy-start.12 = (bf16[3,4,1536]{2,1,0:T(4,128)(2,1)S(1)}, bf16[3,4,1536]{2,1,0:T(4,128)(2,1)}, u32[]{:S(2)}) copy-start(bf16[3,4,1536]{2,1,0:T(4,128)(2,1)} %param.14) | copy-start | bytes 110596
  7.2 526.9 %all-gather.2.cloned.1.call-start = ((), (), s32[]{:S(2)}) async-start(), calls=%async_computation | async-start | bytes 10027008 | tf_op jit(solution)/shard_map/all_gather | solution.py:87
  7.2 53.8 %collective-permute-start.1 = (bf16[192,3,1024]{2,0,1:T(8,128)(2,1)}, bf16[192,3,1024]{2,0,1:T(8,128)(2,1)S(1)}, u32[]{:S(2)}, u32[]{:S(2)}) collective-permute-start(bf16[192,3,1024]{2,0,1:T(8,128)(2,1)} %param.15), channel_id=1, source_target_pairs={{0,2},{2,4},{4,6},{6,8},{8,10},{10,12},{12,14},{14,16},{16,18},{18... | collective-permute-start | bytes 3538952 | tf_op jit(solution)/shard_map/ppermute | solution.py:57
  10.2 53.2 %collective-permute-start = (bf16[192,3,1024]{2,0,1:T(8,128)(2,1)}, bf16[192,3,1024]{2,0,1:T(8,128)(2,1)S(1)}, u32[]{:S(2)}, u32[]{:S(2)}) collective-permute-start(bf16[192,3,1024]{2,0,1:T(8,128)(2,1)} %param.15), channel_id=1, source_target_pairs={{0,30},{2,0},{4,2},{6,4},{8,6},{10,8},{12,10},{14,12},{16,14},{18,... | collective-permute-start | bytes 3538952 | tf_op jit(solution)/shard_map/ppermute | solution.py:59
  61.1 52.0 %copy-start.4 = (bf16[192,3,1024]{2,0,1:T(8,128)(2,1)}, bf16[192,3,1024]{2,0,1:T(8,128)(2,1)S(1)}, u32[]{:S(2)}) copy-start(bf16[192,3,1024]{2,0,1:T(8,128)(2,1)S(1)} %collective-permute-done.1) | copy-start | bytes 3538948
  61.1 52.0 %collective-permute-start.3 = (bf16[192,3,1024]{2,0,1:T(8,128)(2,1)S(1)}, bf16[192,3,1024]{2,0,1:T(8,128)(2,1)S(1)}, u32[]{:S(2)}, u32[]{:S(2)}) collective-permute-start(bf16[192,3,1024]{2,0,1:T(8,128)(2,1)S(1)} %collective-permute-done.1), channel_id=1, source_target_pairs={{0,2},{2,4},{4,6},{6,8},{8,10},{10,12},{12,14},{14,16},{16,18},{18... | collective-permute-start | bytes 3538952 | tf_op jit(solution)/shard_map/ppermute | solution.py:57
  63.4 105.7 %copy-start.8 = (bf16[192,3,1024]{2,0,1:T(8,128)(2,1)}, bf16[192,3,1024]{2,0,1:T(8,128)(2,1)S(1)}, u32[]{:S(2)}) copy-start(bf16[192,3,1024]{2,0,1:T(8,128)(2,1)S(1)} %collective-permute-done) | copy-start | bytes 3538948
  63.4 56.0 %collective-permute-start.2 = (bf16[192,3,1024]{2,0,1:T(8,128)(2,1)S(1)}, bf16[192,3,1024]{2,0,1:T(8,128)(2,1)S(1)}, u32[]{:S(2)}, u32[]{:S(2)}) collective-permute-start(bf16[192,3,1024]{2,0,1:T(8,128)(2,1)S(1)} %collective-permute-done), channel_id=1, source_target_pairs={{0,30},{2,0},{4,2},{6,4},{8,6},{10,8},{12,10},{14,12},{16,14},{18,... | collective-permute-start | bytes 3538952 | tf_op jit(solution)/shard_map/ppermute | solution.py:59
  113.1 51.3 %collective-permute-start.5 = (bf16[192,3,1024]{2,0,1:T(8,128)(2,1)S(1)}, bf16[192,3,1024]{2,0,1:T(8,128)(2,1)S(1)}, u32[]{:S(2)}, u32[]{:S(2)}) collective-permute-start(bf16[192,3,1024]{2,0,1:T(8,128)(2,1)S(1)} %collective-permute-done.3), channel_id=1, source_target_pairs={{0,2},{2,4},{4,6},{6,8},{8,10},{10,12},{12,14},{14,16},{16,18},{18... | collective-permute-start | bytes 3538952 | tf_op jit(solution)/shard_map/ppermute | solution.py:57
  119.4 98.6 %copy-start.6 = (bf16[192,3,1024]{2,0,1:T(8,128)(2,1)}, bf16[192,3,1024]{2,0,1:T(8,128)(2,1)S(1)}, u32[]{:S(2)}) copy-start(bf16[192,3,1024]{2,0,1:T(8,128)(2,1)S(1)} %collective-permute-done.2) | copy-start | bytes 3538948
  119.5 49.8 %collective-permute-start.4 = (bf16[192,3,1024]{2,0,1:T(8,128)(2,1)S(1)}, bf16[192,3,1024]{2,0,1:T(8,128)(2,1)}, u32[]{:S(2)}, u32[]{:S(2)}) collective-permute-start(bf16[192,3,1024]{2,0,1:T(8,128)(2,1)S(1)} %collective-permute-done.2), channel_id=1, source_target_pairs={{0,30},{2,0},{4,2},{6,4},{8,6},{10,8},{12,10},{14,12},{16,14},{18,... | collective-permute-start | bytes 3538952 | tf_op jit(solution)/shard_map/ppermute | solution.py:59
  164.4 53.7 %copy-start.2 = (bf16[192,3,1024]{2,0,1:T(8,128)(2,1)}, bf16[192,3,1024]{2,0,1:T(8,128)(2,1)S(1)}, u32[]{:S(2)}) copy-start(bf16[192,3,1024]{2,0,1:T(8,128)(2,1)S(1)} %collective-permute-done.5) | copy-start | bytes 3538948
  164.4 51.1 %collective-permute-start.7 = (bf16[192,3,1024]{2,0,1:T(8,128)(2,1)S(1)}, bf16[192,3,1024]{2,0,1:T(8,128)(2,1)}, u32[]{:S(2)}, u32[]{:S(2)}) collective-permute-start(bf16[192,3,1024]{2,0,1:T(8,128)(2,1)S(1)} %collective-permute-done.5), channel_id=1, source_target_pairs={{0,2},{2,4},{4,6},{6,8},{8,10},{10,12},{12,14},{14,16},{16,18},{18... | collective-permute-start | bytes 3538952 | tf_op jit(solution)/shard_map/ppermute | solution.py:57
  168.7 50.2 %copy-start.13 = (f32[2,1024]{1,0:T(2,128)S(1)}, f32[2,1024]{1,0:T(2,128)}, u32[]{:S(2)}) copy-start(f32[2,1024]{1,0:T(2,128)} %param.16) | copy-start | bytes 24580
  168.7 50.2 %copy-start.1 = (bf16[192,3,1024]{2,0,1:T(8,128)(2,1)S(1)}, bf16[192,3,1024]{2,0,1:T(8,128)(2,1)}, u32[]{:S(2)}) copy-start(bf16[192,3,1024]{2,0,1:T(8,128)(2,1)} %param.15) | copy-start | bytes 3538948
  169.2 51.5 %collective-permute-start.6 = (bf16[192,3,1024]{2,0,1:T(8,128)(2,1)}, bf16[192,3,1024]{2,0,1:T(8,128)(2,1)}, u32[]{:S(2)}, u32[]{:S(2)}) collective-permute-start(bf16[192,3,1024]{2,0,1:T(8,128)(2,1)} %collective-permute-done.4), channel_id=1, source_target_pairs={{0,30},{2,0},{4,2},{6,4},{8,6},{10,8},{12,10},{14,12},{16,14},{18,... | collective-permute-start | bytes 3538952 | tf_op jit(solution)/shard_map/ppermute | solution.py:59
  215.5 51.2 %collective-permute-start.9 = (bf16[192,3,1024]{2,0,1:T(8,128)(2,1)}, bf16[192,3,1024]{2,0,1:T(8,128)(2,1)}, u32[]{:S(2)}, u32[]{:S(2)}) collective-permute-start(bf16[192,3,1024]{2,0,1:T(8,128)(2,1)} %collective-permute-done.7), channel_id=1, source_target_pairs={{0,2},{2,4},{4,6},{6,8},{8,10},{10,12},{12,14},{14,16},{16,18},{18... | collective-permute-start | bytes 3538952 | tf_op jit(solution)/shard_map/ppermute | solution.py:57
  218.9 1.3 copy-start.9
  220.2 25.1 %copy-start.5 = (bf16[192,3,1024]{2,0,1:T(8,128)(2,1)S(1)}, bf16[192,3,1024]{2,0,1:T(8,128)(2,1)}, u32[]{:S(2)}) copy-start(bf16[192,3,1024]{2,0,1:T(8,128)(2,1)} %copy-done.4) | copy-start | bytes 3538948
  220.7 48.5 %copy-start.7 = (bf16[192,3,1024]{2,0,1:T(8,128)(2,1)S(1)}, bf16[192,3,1024]{2,0,1:T(8,128)(2,1)}, u32[]{:S(2)}) copy-start(bf16[192,3,1024]{2,0,1:T(8,128)(2,1)} %copy-done.6) | copy-start | bytes 3538948
  220.7 51.3 %collective-permute-start.8 = (bf16[192,3,1024]{2,0,1:T(8,128)(2,1)}, bf16[192,3,1024]{2,0,1:T(8,128)(2,1)S(1)}, u32[]{:S(2)}, u32[]{:S(2)}) collective-permute-start(bf16[192,3,1024]{2,0,1:T(8,128)(2,1)} %collective-permute-done.6), channel_id=1, source_target_pairs={{0,30},{2,0},{4,2},{6,4},{8,6},{10,8},{12,10},{14,12},{16,14},{18,... | collective-permute-start | bytes 3538952 | tf_op jit(solution)/shard_map/ppermute | solution.py:59
  266.7 50.4 %collective-permute-start.11 = (bf16[192,3,1024]{2,0,1:T(8,128)(2,1)}, bf16[192,3,1024]{2,0,1:T(8,128)(2,1)S(1)}, u32[]{:S(2)}, u32[]{:S(2)}) collective-permute-start(bf16[192,3,1024]{2,0,1:T(8,128)(2,1)} %collective-permute-done.9), channel_id=1, source_target_pairs={{0,2},{2,4},{4,6},{6,8},{8,10},{10,12},{12,14},{14,16},{16,18},{18... | collective-permute-start | bytes 3538952 | tf_op jit(solution)/shard_map/ppermute | solution.py:57
  270.2 26.4 %copy-start.3 = (bf16[192,3,1024]{2,0,1:T(8,128)(2,1)S(1)}, bf16[192,3,1024]{2,0,1:T(8,128)(2,1)}, u32[]{:S(2)}) copy-start(bf16[192,3,1024]{2,0,1:T(8,128)(2,1)} %copy-done.2) | copy-start | bytes 3538948
  272.0 51.5 %collective-permute-start.10 = (bf16[192,3,1024]{2,0,1:T(8,128)(2,1)S(1)}, bf16[192,3,1024]{2,0,1:T(8,128)(2,1)S(1)}, u32[]{:S(2)}, u32[]{:S(2)}) collective-permute-start(bf16[192,3,1024]{2,0,1:T(8,128)(2,1)S(1)} %collective-permute-done.8), channel_id=1, source_target_pairs={{0,30},{2,0},{4,2},{6,4},{8,6},{10,8},{12,10},{14,12},{16,14},{18,... | collective-permute-start | bytes 3538952 | tf_op jit(solution)/shard_map/ppermute | solution.py:59
  317.2 51.3 %collective-permute-start.13 = (bf16[192,3,1024]{2,0,1:T(8,128)(2,1)S(1)}, bf16[192,3,1024]{2,0,1:T(8,128)(2,1)S(1)}, u32[]{:S(2)}, u32[]{:S(2)}) collective-permute-start(bf16[192,3,1024]{2,0,1:T(8,128)(2,1)S(1)} %collective-permute-done.11), channel_id=1, source_target_pairs={{0,2},{2,4},{4,6},{6,8},{8,10},{10,12},{12,14},{14,16},{16,18},{18... | collective-permute-start | bytes 3538952 | tf_op jit(solution)/shard_map/ppermute | solution.py:57
  323.5 52.7 %collective-permute-start.12 = (bf16[192,3,1024]{2,0,1:T(8,128)(2,1)S(1)}, bf16[192,3,1024]{2,0,1:T(8,128)(2,1)S(1)}, u32[]{:S(2)}, u32[]{:S(2)}) collective-permute-start(bf16[192,3,1024]{2,0,1:T(8,128)(2,1)S(1)} %collective-permute-done.10), channel_id=1, source_target_pairs={{0,30},{2,0},{4,2},{6,4},{8,6},{10,8},{12,10},{14,12},{16,14},{18,... | collective-permute-start | bytes 3538952 | tf_op jit(solution)/shard_map/ppermute | solution.py:59
  368.5 25.3 %collective-permute-start.14 = (bf16[192,3,1024]{2,0,1:T(8,128)(2,1)S(1)}, bf16[192,3,1024]{2,0,1:T(8,128)(2,1)}, u32[]{:S(2)}, u32[]{:S(2)}) collective-permute-start(bf16[192,3,1024]{2,0,1:T(8,128)(2,1)S(1)} %collective-permute-done.13), channel_id=1, source_target_pairs={{0,2},{2,4},{4,6},{6,8},{8,10},{10,12},{12,14},{14,16},{16,18},{18... | collective-permute-start | bytes 3538952 | tf_op jit(solution)/shard_map/ppermute | solution.py:57
  408.7 2.5 copy-start.11
  408.8 45.2 %copy-start.14 = (s32[4]{0:T(128)S(1)}, s32[4]{0:T(128)}, u32[]{:S(2)}) copy-start(s32[4]{0:T(128)} %param.18) | copy-start | bytes 52
  410.1 186.5 %all-reduce.3.cloned.1.call-start = ((), (), s32[]{:S(2)}) async-start(), calls=%async_computation.1 | async-start | bytes 1572864 | tf_op jit(solution)/shard_map/psum | solution.py:118
  568.4 8.9 %slice-start = ((s8[6291456]{0:T(1024)(128)(4,1)}), s8[4194304]{0:T(1024)(128)(4,1)S(1)}, s32[]{:S(2)}) async-start(s8[6291456]{0:T(1024)(128)(4,1)} %bitcast.182), calls=%async_computation.2 | async-start | bytes 8388608
  569.2 8.1 %slice-start.1 = ((s8[6291456]{0:T(1024)(128)(4,1)}), s8[2097152]{0:T(1024)(128)(4,1)S(1)}, s32[]{:S(2)}) async-start(s8[6291456]{0:T(1024)(128)(4,1)} %bitcast.182), calls=%async_computation.3 | async-start | bytes 4194304
  577.3 1.9 copy-start.15
  577.3 19.2 %copy-start = (bf16[4,32,1536]{2,1,0:T(8,128)(2,1)S(1)}, bf16[4,32,1536]{2,1,0:T(8,128)(2,1)}, u32[]{:S(2)}) copy-start(bf16[4,32,1536]{2,1,0:T(8,128)(2,1)} %param.10) | copy-start | bytes 1179652
  577.4 19.2 %copy-start.10 = (f32[4,32,1536]{2,1,0:T(8,128)S(1)}, f32[4,32,1536]{2,1,0:T(8,128)}, u32[]{:S(2)}) copy-start(f32[4,32,1536]{2,1,0:T(8,128)} %param.13) | copy-start | bytes 2359300
Sparse Core Ops, SparseCore 0:
  410.2 123.8 all-gather.1
  579.4 17.1 all-reduce.2
